TPU v7x, 256 devices: a whole 4x4x8 slice. The times are simulated.
256 devices in a mesh: gx: 16 (over z, core), gy: 4 (over x), gz: 4 (over y).
Axes of the slice: x: 4, y: 4, z: 8, core: 2. Of those that a mesh axis runs over, the one named last changes fastest.
Arguments:
- velocity: float32 [3, 1024, 128, 512], P(None, 'gx', 'gz', 'gy'), may hold values from -6 to 6
- tile_turbine: int32 [16, 4, 4, 2], P('gx', 'gz', 'gy'), may hold values from 0 to 63
- tile_plane: int32 [16, 4, 4, 2], P('gx', 'gz', 'gy'), may hold values from 0 to 63
- tile_weight: bfloat16 [16, 4, 4, 2, 384, 4096], P('gx', 'gz', 'gy'), may hold values from -0.09375 to 0.09375
- chord: float32 [64, 384], replicated, may hold values from 0.25 to 1
Outputs:
- predicted: float32 [3, 1024, 128, 512], P(None, 'gx', 'gz', 'gy')
- forces: float32 [64, 1152], replicated
All inputs are finite; a program needn't handle non-finite values.
Results may differ from a plain program's by a relative error of at most 0.0032.
Values sent between devices are 32-bit elements; how exact they have to be, the bound alone decides.
No kernel may reach another device: no remote copies, remote signals or barrier semaphores. Data moves between devices by JAX's collectives and lax.ppermute only.
A program may use at most 128 MiB of HBM per device.

v0:
```python
import jax
import jax.numpy as jnp
from jax import lax
from jax.sharding import PartitionSpec as P

DIRS = (-3, -1, -2)


def padded_2(block, sides, width):
    for axis, dim in sides:
        count = lax.axis_size(axis)
        forward = [(i, i + 1) for i in range(count - 1)]
        backward = [(target, source) for source, target in forward]
        low = lax.ppermute(
            lax.slice_in_dim(block, block.shape[dim] - width, None, axis=dim), axis, forward
        )
        high = lax.ppermute(lax.slice_in_dim(block, 0, width, axis=dim), axis, backward)
        block = jnp.concatenate([low, block, high], axis=dim)
    return block


def shifted(p, axis, step):
    idx = [slice(1, -1), slice(1, -1), slice(1, -1)]
    idx[axis + 3] = slice(1 + step, p.shape[axis] - 1 + step)
    lead = [slice(None)] * (p.ndim - 3)
    return p[tuple(lead + idx)]


def strain_viscosity(p):
    grads = [
        [0.5 * (shifted(p[c], DIRS[d], 1) - shifted(p[c], DIRS[d], -1)) for d in range(3)]
        for c in range(3)
    ]
    total = jnp.zeros_like(grads[0][0])
    for c in range(3):
        for d in range(3):
            strain = 0.5 * (grads[c][d] + grads[d][c])
            total = total + strain * strain
    return 0.05 + 1.0 * jnp.sqrt(2.0 * total + 1e-06)


def advance(padded, nu_padded):
    nu_here = shifted(nu_padded, -1, 0)
    result = []
    for c in range(3):
        center = shifted(padded[c], -1, 0)
        advect = jnp.zeros_like(center)
        spread = jnp.zeros_like(center)
        for d in range(3):
            upper = shifted(padded[c], DIRS[d], 1)
            lower = shifted(padded[c], DIRS[d], -1)
            advect = advect + shifted(padded[d], -1, 0) * 0.5 * (upper - lower)
            nu_up = 0.5 * (nu_here + shifted(nu_padded, DIRS[d], 1))
            nu_low = 0.5 * (nu_here + shifted(nu_padded, DIRS[d], -1))
            spread = spread + nu_up * (upper - center) - nu_low * (center - lower)
        result.append(center + 0.25 * (spread - advect))
    return jnp.stack(result)


def actuate(velocity_probe, coef):
    rows = velocity_probe.shape[0]
    parts = velocity_probe.reshape(rows, 3, -1)
    magnitude = jnp.sqrt(jnp.sum(parts * parts, axis=1) + 1e-06)
    return (-2.0 * coef[:, None, :] * magnitude[:, None, :] * parts).reshape(rows, -1)


def body(velocity, tile_turbine, tile_plane, tile_weight, chord):
    cx = velocity.shape[1]
    vertical_coord = velocity.shape[2]
    spanwise_coord = velocity.shape[3]
    tile_count = tile_turbine.shape[3]
    actuator_count = tile_weight.shape[4]
    nturb = chord.shape[0]
    turbine_list = tile_turbine.reshape(tile_count)
    rotor_planes = tile_plane.reshape(tile_count)
    spread_weights = tile_weight.reshape(
        tile_count, actuator_count, vertical_coord * spanwise_coord
    )
    flat = velocity.reshape(3, cx, vertical_coord * spanwise_coord)
    picks = (rotor_planes[:, None] == jnp.arange(cx, dtype=jnp.int32)[None, :]).astype(jnp.float32)
    tiles = jnp.einsum("sx,cxq->scq", picks, flat, precision=lax.Precision.HIGHEST).astype(
        jnp.bfloat16
    )
    block_local = jnp.einsum(
        "spq,scq->scp", spread_weights, tiles, preferred_element_type=jnp.float32
    )
    owning_block = (turbine_list[:, None] == jnp.arange(nturb, dtype=jnp.int32)[None, :]).astype(
        jnp.float32
    )
    partial_sample = jnp.einsum(
        "yr,yw->rw",
        owning_block,
        block_local.reshape(tile_count, -1),
        precision=lax.Precision.HIGHEST,
    )
    rows = lax.axis_size("gx")
    per_row = nturb // rows
    received = lax.all_to_all(
        partial_sample.reshape(rows, per_row, -1), "gx", split_axis=0, concat_axis=0, tiled=True
    )
    owned = lax.psum(jnp.sum(received, axis=0), ("gy", "gz"))
    owned_coef = lax.dynamic_slice_in_dim(chord, lax.axis_index("gx") * per_row, per_row, 0)
    forces = lax.all_gather(actuate(owned, owned_coef), "gx", axis=0, tiled=True)
    tile_force = jnp.dot(owning_block, forces, precision=lax.Precision.HIGHEST).astype(jnp.bfloat16)
    forces_sent = jnp.einsum(
        "axz,ahx->ahz",
        spread_weights,
        tile_force.reshape(tile_count, 3, actuator_count),
        preferred_element_type=jnp.float32,
    )
    impulse = jnp.einsum(
        "sx,scq->cxq", picks, forces_sent, precision=lax.Precision.HIGHEST
    ).reshape(3, cx, vertical_coord, spanwise_coord)
    padded = padded_2(velocity, (("gx", 1), ("gy", 3), ("gz", 2)), 1)
    viscosity = strain_viscosity(padded)
    nu_padded = padded_2(viscosity, (("gx", 0), ("gy", 2), ("gz", 1)), 1)
    predicted = advance(padded, nu_padded) + impulse
    return (predicted, forces)


def solution(mesh):
    placed = (
        P(None, "gx", "gz", "gy"),
        P("gx", "gz", "gy", None),
        P("gx", "gz", "gy", None),
        P("gx", "gz", "gy", None, None, None),
        P(),
    )
    return jax.shard_map(
        body,
        mesh=mesh,
        in_specs=placed,
        out_specs=(P(None, "gx", "gz", "gy"), P()),
        check_vma=False,
    )
```

profile of v0, /device:TPU:1, one launch (start us, length us, event | category | flops | bytes accessed | tf_op | source)
XLA Modules:
  0.0 237.4 jit_solution(2430142811792057786)
XLA Ops:
  0.6 0.8 fusion.31
  1.5 4.9 %collective-permute-start = (f32[3,1,32,128]{3,2,1,0:T(8,128)S(1)}, f32[3,1,32,128]{3,2,1,0:T(8,128)S(1)}, u32[]{:S(2)}, u32[]{:S(2)}) collective-permute-start(f32[3,1,32,128]{3,2,1,0:T(8,128)S(1)} %get-tuple-element.16), channel_id=1, source_target_pairs={{0,16},{16,32},{32,48},{48,64},{64,80},{80,96},{96,112},{112,128},... | collective-permute-start | bytes 147464 | tf_op jit(solution)/shard_map/ppermute | solution.py:14
  6.4 1.9 collective-permute-start.1
  8.3 2.2 constant_dynamic-update-slice_fusion.1
  10.5 1.3 collective-permute-done.1
  11.8 3.9 %fusion.30 = (f32[3,66,32,1]{3,2,1,0:T(8,128)}, f32[3,66,32,1]{3,2,1,0:T(8,128)}) fusion(f32[3,66,32,128]{3,2,1,0:T(8,128)S(1)} %constant_dynamic-update-slice_fusion), kind=kLoop, calls=%fused_computation.87 | loop fusion | bytes 101376 | tf_op jit(solution)/shard_map/slice | solution.py:15
  15.7 2.8 %copy.29 = f32[3,66,32,1]{1,2,3,0:T(8,128)S(1)} copy(f32[3,66,32,1]{3,2,1,0:T(8,128)} %get-tuple-element.13) | data formatting | bytes 50688 | tf_op jit(solution)/shard_map/slice | solution.py:15
  18.5 3.1 %collective-permute-start.2 = (f32[3,66,32,1]{1,2,3,0:T(8,128)S(1)}, f32[3,66,32,1]{1,2,3,0:T(8,128)S(1)}, u32[]{:S(2)}, u32[]{:S(2)}) collective-permute-start(f32[3,66,32,1]{1,2,3,0:T(8,128)S(1)} %copy.29), channel_id=1, source_target_pairs={{0,4},{4,8},{8,12},{1,5},{5,9},{9,13},{2,6},{6,10},{10,14},{3,7},{... | collective-permute-start | bytes 76040 | tf_op jit(solution)/shard_map/ppermute | solution.py:14
  21.6 2.8 %copy.30 = f32[3,66,32,1]{1,2,3,0:T(8,128)S(1)} copy(f32[3,66,32,1]{3,2,1,0:T(8,128)} %get-tuple-element.14) | data formatting | bytes 50688 | tf_op jit(solution)/shard_map/slice | solution.py:17
  24.4 1.3 collective-permute-start.3
  25.7 4.6 %reshape.47 = f32[3,64,4096]{2,1,0:T(8,128)} reshape(f32[3,64,32,128]{3,2,1,0:T(8,128)} %param.5) | data formatting | bytes 6291456 | tf_op jit(solution)/shard_map/reshape | solution.py:79
  30.3 2.7 %copy.31 = f32[3,66,32,1]{3,2,1,0:T(8,128)} copy(f32[3,66,32,1]{1,2,3,0:T(8,128)S(1)} %collective-permute-done.2) | data formatting | bytes 50688 | tf_op jit(solution)/shard_map/ppermute | solution.py:14
  33.0 2.7 %copy.32 = f32[3,66,32,1]{3,2,1,0:T(8,128)} copy(f32[3,66,32,1]{1,2,3,0:T(8,128)S(1)} %collective-permute-done.3) | data formatting | bytes 50688 | tf_op jit(solution)/shard_map/ppermute | solution.py:17
  35.7 3.4 %pad_maximum_fusion.22 = (f32[3,66,1,130]{3,2,1,0:T(1,128)S(1)}, f32[3,66,1,130]{3,2,1,0:T(1,128)S(1)}) fusion(f32[3,66,32,1]{3,2,1,0:T(8,128)} %copy.32, f32[3,66,32,128]{3,2,1,0:T(8,128)S(1)} %constant_dynamic-update-slice_fusion, f32[3,66,32,1]{3,2,1,0:T(8,128)} %copy.31), kind=kLoop, calls=%fused_computation.60 | loop fusion | flops 102960 | bytes 3500640 | tf_op jit(solution)/shard_map/slice | solution.py:15
  39.1 3.3 %collective-permute-start.4 = (f32[3,66,1,130]{3,2,1,0:T(1,128)S(1)}, f32[3,66,1,130]{3,2,1,0:T(1,128)S(1)}, u32[]{:S(2)}, u32[]{:S(2)}) collective-permute-start(f32[3,66,1,130]{3,2,1,0:T(1,128)S(1)} %get-tuple-element.6), channel_id=1, source_target_pairs={{0,1},{1,2},{2,3},{4,5},{5,6},{6,7},{8,9},{9,10},{10,11},{12,13},{... | collective-permute-start | bytes 308888 | tf_op jit(solution)/shard_map/ppermute | solution.py:14
  42.5 1.3 collective-permute-start.5
  43.8 1.1 convolution_convert_fusion
  44.9 0.9 collective-permute-done.4
  45.8 4.1 %collective-permute-done.5 = f32[3,66,1,130]{3,2,1,0:T(1,128)S(1)} collective-permute-done((f32[3,66,1,130]{3,2,1,0:T(1,128)S(1)}, f32[3,66,1,130]{3,2,1,0:T(1,128)S(1)}, u32[]{:S(2)}, u32[]{:S(2)}) %collective-permute-start.5) | collective-permute-done | bytes 102992 | tf_op jit(solution)/shard_map/ppermute | solution.py:17
  49.9 4.0 %pad_maximum_fusion = f32[3,66,34,130]{3,2,1,0:T(8,128)S(1)} fusion(f32[3,66,1,130]{3,2,1,0:T(1,128)S(1)} %collective-permute-done.5, f32[3,66,32,1]{3,2,1,0:T(8,128)S(1)} %copy-done.7, f32[3,66,32,128]{3,2,1,0:T(8,128)S(1)} %constant_dynamic-update-slice_fusion, f32[3,66,32,1]{3,2,1,0:T(8,128)S(1)} %copy-done.6, f32[3,66,1,130]{3,2,1,0:T(1,128)S(1)} %collective-permute-done.4), kind=kLoop, calls=%fused_computation | loop fusion | flops 3500640 | bytes 7001280 | tf_op jit(solution)/shard_map/concatenate | solution.py:18
  53.9 0.5 slice_bitcast_fusion.1
  54.5 4.8 %sqrt_add_fusion = f32[64,32,128]{2,1,0:T(8,128)S(1)} fusion(f32[66,34,130]{2,1,0:T(8,128)S(1)} %get-tuple-element.10, f32[66,34,130]{2,1,0:T(8,128)S(1)} %get-tuple-element.8, f32[66,34,130]{2,1,0:T(8,128)S(1)} %get-tuple-element.9), kind=kLoop, calls=%fused_computation.45 | loop fusion | flops 9961472 | bytes 19922944 | tf_op jit(solution)/shard_map/add | solution.py:39
  59.3 1.9 collective-permute-start.6
  61.2 5.5 %collective-permute-start.7 = (f32[1,32,128]{2,1,0:T(8,128)S(1)}, f32[1,32,128]{2,1,0:T(8,128)S(1)}, u32[]{:S(2)}, u32[]{:S(2)}) collective-permute-start(f32[1,32,128]{2,1,0:T(8,128)S(1)} %get-tuple-element.19), channel_id=1, source_target_pairs={{0,16},{16,32},{32,48},{48,64},{64,80},{80,96},{96,112},{112,128},... | collective-permute-start | bytes 49160 | tf_op jit(solution)/shard_map/ppermute | solution.py:14
  66.8 4.5 %fusion.2 = f32[2,3,384]{2,1,0:T(4,128)S(1)} fusion(bf16[1,1,1,2,384,4096]{5,4,3,2,1,0:T(8,128)(2,1)} %param.8, bf16[2,3,4096]{2,0,1:T(2,128)(2,1)S(1)} %convolution_convert_fusion), kind=kOutput, calls=%fused_computation.3 | convolution fusion | flops 18874368 | bytes 6349824 | tf_op jit(solution)/shard_map/spq,scq->scp/dot_general | solution.py:84
  71.4 1.7 fusion.32
  73.1 1.9 copy.33
  75.0 1.3 collective-permute-start.8
  76.3 1.9 copy.35
  78.2 4.6 %collective-permute-start.9 = (f32[66,32,1]{0,1,2:T(8,128)S(1)}, f32[66,32,1]{0,1,2:T(8,128)S(1)}, u32[]{:S(2)}, u32[]{:S(2)}) collective-permute-start(f32[66,32,1]{0,1,2:T(8,128)S(1)} %copy.35), channel_id=1, source_target_pairs={{0,4},{4,8},{8,12},{1,5},{5,9},{9,13},{2,6},{6,10},{10,14},{3,7},{... | collective-permute-start | bytes 25352 | tf_op jit(solution)/shard_map/ppermute | solution.py:14
  82.8 1.9 copy.34
  84.7 1.9 copy.36
  86.6 1.9 pad_maximum_fusion.23
  88.5 1.3 collective-permute-start.10
  89.8 4.0 %collective-permute-start.11 = (f32[66,1,130]{2,1,0:T(1,128)S(1)}, f32[66,1,130]{2,1,0:T(1,128)S(1)}, u32[]{:S(2)}, u32[]{:S(2)}) collective-permute-start(f32[66,1,130]{2,1,0:T(1,128)S(1)} %get-tuple-element.11), channel_id=1, source_target_pairs={{0,1},{1,2},{2,3},{4,5},{5,6},{6,7},{8,9},{9,10},{10,11},{12,13},{... | collective-permute-start | bytes 102968 | tf_op jit(solution)/shard_map/ppermute | solution.py:14
  94.2 0.8 copy.40
  95.1 7.6 %all-to-all-start = ((f32[16,4,1152]{2,1,0:T(4,128)}), f32[16,4,1152]{2,1,0:T(4,128)S(1)}, u32[]{:S(2)}, u32[]{:S(2)}) async-start(f32[16,4,1152]{2,1,0:T(4,128)} %copy.40), calls=%async_computation | async-start | bytes 589824 | tf_op jit(solution)/shard_map/all_to_all | solution.py:98
  102.7 17.9 %add_bitcast_fusion.2 = f32[1,64,32,128]{3,2,1,0:T(8,128)} fusion(f32[66,34,130]{2,1,0:T(8,128)} %copy-done.2, f32[66,34,130]{2,1,0:T(8,128)S(1)} %get-tuple-element.8, f32[66,34,130]{2,1,0:T(8,128)} %copy-done, f32[64,32,128]{2,1,0:T(8,128)} %copy-done.4, f32[1,32,128]{2,1,0:T(8,128)S(1)} %collective-permute-done.6, ...), kind=kLoop, calls=%fused_computation.44 | loop fusion | flops 15990784 | bytes 11652640 | tf_op jit(solution)/shard_map/stack | solution.py:57
  120.7 7.1 %add_bitcast_fusion.1 = f32[1,64,32,128]{3,2,1,0:T(8,128)} fusion(f32[66,34,130]{2,1,0:T(8,128)S(1)} %get-tuple-element.8, f32[66,34,130]{2,1,0:T(8,128)S(1)} %copy-done.3, f32[66,34,130]{2,1,0:T(8,128)S(1)} %copy-done.1, f32[64,32,128]{2,1,0:T(8,128)S(1)} %copy-done.5, f32[1,32,128]{2,1,0:T(8,128)S(1)} %collective-permute-done.6, ...), kind=kLoop, calls=%fused_computation.43 | loop fusion | flops 15990784 | bytes 11652640 | tf_op jit(solution)/shard_map/stack | solution.py:57
  127.9 7.1 %add_bitcast_fusion = f32[1,64,32,128]{3,2,1,0:T(8,128)} fusion(f32[66,34,130]{2,1,0:T(8,128)S(1)} %copy-done.1, f32[66,34,130]{2,1,0:T(8,128)S(1)} %copy-done.3, f32[66,34,130]{2,1,0:T(8,128)S(1)} %get-tuple-element.8, f32[64,32,128]{2,1,0:T(8,128)S(1)} %copy-done.5, f32[1,32,128]{2,1,0:T(8,128)S(1)} %collective-permute-done.6, ...), kind=kLoop, calls=%fused_computation.42 | loop fusion | flops 15990784 | bytes 11652640 | tf_op jit(solution)/shard_map/stack | solution.py:57
  135.0 59.5 %psum.7 = f32[4,1152]{1,0:T(4,128)S(1)} all-reduce(f32[4,1152]{1,0:T(4,128)S(1)} %reduce_sum.18), channel_id=1, replica_groups=mesh['gx'=16,'gy'=4,'gz'=4] {'gy','gz'}, use_global_device_ids=true, to_apply=%region_1.0 | all-reduce | flops 4608 | bytes 36864 | tf_op jit(solution)/shard_map/psum | solution.py:101
  194.5 0.7 sqrt_multiply_fusion
  195.3 32.2 %all-gather = f32[16,4,1152]{2,1,0:T(4,128)S(1)} all-gather(f32[1,4,1152]{2,1,0:T(4,128)S(1)} %multiply_bitcast_fusion), channel_id=1, replica_groups=mesh['gx'=16,'gy'=4,'gz'=4] {'gx'}, dimensions={0}, use_global_device_ids=true | all-gather | bytes 313344 | tf_op jit(solution)/shard_map/all_gather | solution.py:103
  227.9 3.7 %fusion = f32[2,3,4096]{2,1,0:T(4,128)S(1)} fusion(bf16[2,3,384]{2,1,0:T(4,128)(2,1)S(1)} %reshape.50, bf16[1,1,1,2,384,4096]{5,4,3,2,1,0:T(8,128)(2,1)} %param.8), kind=kOutput, calls=%fused_computation.1 | convolution fusion | flops 18874368 | bytes 6394368 | tf_op jit(solution)/shard_map/axz,ahx->ahz/dot_general | solution.py:105
  231.6 1.5 fusion.16
  233.2 0.5 copy.42
  233.7 0.6 copy-done.11
  235.0 2.4 %bitcast_add_fusion = f32[3,64,32,128]{3,2,1,0:T(8,128)} fusion(f32[1,64,32,128]{3,2,1,0:T(8,128)S(1)} %copy-done.13, f32[1,64,32,128]{3,2,1,0:T(8,128)S(1)} %copy-done.12, f32[1,64,32,128]{3,2,1,0:T(8,128)S(1)} %copy-done.11, f32[3,64,32,128]{3,2,1,0:T(8,128)S(1)} %bitcast.42), kind=kLoop, calls=%fused_computation.6 | loop fusion | flops 2359296 | bytes 9437184 | tf_op jit(solution)/shard_map/add | solution.py:117
  (58 shorter events, 1.7 us)
Async XLA Ops:
  1.5 6.9 %collective-permute-start = (f32[3,1,32,128]{3,2,1,0:T(8,128)S(1)}, f32[3,1,32,128]{3,2,1,0:T(8,128)S(1)}, u32[]{:S(2)}, u32[]{:S(2)}) collective-permute-start(f32[3,1,32,128]{3,2,1,0:T(8,128)S(1)} %get-tuple-element.16), channel_id=1, source_target_pairs={{0,16},{16,32},{32,48},{48,64},{64,80},{80,96},{96,112},{112,128},... | collective-permute-start | bytes 147464 | tf_op jit(solution)/shard_map/ppermute | solution.py:14
  6.4 5.4 %collective-permute-start.1 = (f32[3,1,32,128]{3,2,1,0:T(8,128)S(1)}, f32[3,1,32,128]{3,2,1,0:T(8,128)S(1)}, u32[]{:S(2)}, u32[]{:S(2)}) collective-permute-start(f32[3,1,32,128]{3,2,1,0:T(8,128)S(1)} %get-tuple-element.15), channel_id=1, source_target_pairs={{16,0},{32,16},{48,32},{64,48},{80,64},{96,80},{112,96},{128,112},... | collective-permute-start | bytes 147464 | tf_op jit(solution)/shard_map/ppermute | solution.py:17
  18.5 11.8 %collective-permute-start.2 = (f32[3,66,32,1]{1,2,3,0:T(8,128)S(1)}, f32[3,66,32,1]{1,2,3,0:T(8,128)S(1)}, u32[]{:S(2)}, u32[]{:S(2)}) collective-permute-start(f32[3,66,32,1]{1,2,3,0:T(8,128)S(1)} %copy.29), channel_id=1, source_target_pairs={{0,4},{4,8},{8,12},{1,5},{5,9},{9,13},{2,6},{6,10},{10,14},{3,7},{... | collective-permute-start | bytes 76040 | tf_op jit(solution)/shard_map/ppermute | solution.py:14
  24.4 8.6 %collective-permute-start.3 = (f32[3,66,32,1]{1,2,3,0:T(8,128)S(1)}, f32[3,66,32,1]{1,2,3,0:T(8,128)S(1)}, u32[]{:S(2)}, u32[]{:S(2)}) collective-permute-start(f32[3,66,32,1]{1,2,3,0:T(8,128)S(1)} %copy.30), channel_id=1, source_target_pairs={{4,0},{8,4},{12,8},{5,1},{9,5},{13,9},{6,2},{10,6},{14,10},{7,3},{... | collective-permute-start | bytes 76040 | tf_op jit(solution)/shard_map/ppermute | solution.py:17
  35.7 8.1 %copy-start.10 = (f32[3,64,4096]{2,1,0:T(8,128)S(1)}, f32[3,64,4096]{2,1,0:T(8,128)}, u32[]{:S(2)}) copy-start(f32[3,64,4096]{2,1,0:T(8,128)} %reshape.47) | copy-start | bytes 9437188
  35.7 8.1 %copy-start.16 = (s32[1,1,1,2]{3,2,1,0:T(1,128)S(1)}, s32[1,1,1,2]{3,2,1,0:T(1,128)}, u32[]{:S(2)}) copy-start(s32[1,1,1,2]{3,2,1,0:T(1,128)} %param.7) | copy-start | bytes 28
  35.7 14.2 %copy-start.6 = (f32[3,66,32,1]{3,2,1,0:T(8,128)S(1)}, f32[3,66,32,1]{3,2,1,0:T(8,128)}, u32[]{:S(2)}) copy-start(f32[3,66,32,1]{3,2,1,0:T(8,128)} %copy.31) | copy-start | bytes 76036
  35.7 14.2 %copy-start.7 = (f32[3,66,32,1]{3,2,1,0:T(8,128)S(1)}, f32[3,66,32,1]{3,2,1,0:T(8,128)}, u32[]{:S(2)}) copy-start(f32[3,66,32,1]{3,2,1,0:T(8,128)} %copy.32) | copy-start | bytes 76036
  39.1 6.6 %collective-permute-start.4 = (f32[3,66,1,130]{3,2,1,0:T(1,128)S(1)}, f32[3,66,1,130]{3,2,1,0:T(1,128)S(1)}, u32[]{:S(2)}, u32[]{:S(2)}) collective-permute-start(f32[3,66,1,130]{3,2,1,0:T(1,128)S(1)} %get-tuple-element.6), channel_id=1, source_target_pairs={{0,1},{1,2},{2,3},{4,5},{5,6},{6,7},{8,9},{9,10},{10,11},{12,13},{... | collective-permute-start | bytes 308888 | tf_op jit(solution)/shard_map/ppermute | solution.py:14
  42.5 7.4 %collective-permute-start.5 = (f32[3,66,1,130]{3,2,1,0:T(1,128)S(1)}, f32[3,66,1,130]{3,2,1,0:T(1,128)S(1)}, u32[]{:S(2)}, u32[]{:S(2)}) collective-permute-start(f32[3,66,1,130]{3,2,1,0:T(1,128)S(1)} %get-tuple-element.7), channel_id=1, source_target_pairs={{1,0},{2,1},{3,2},{5,4},{6,5},{7,6},{9,8},{10,9},{11,10},{13,12},{... | collective-permute-start | bytes 308888 | tf_op jit(solution)/shard_map/ppermute | solution.py:17
  54.4 4.8 %copy-start = (f32[66,34,130]{2,1,0:T(8,128)}, f32[66,34,130]{2,1,0:T(8,128)S(1)}, u32[]{:S(2)}) copy-start(f32[66,34,130]{2,1,0:T(8,128)S(1)} %get-tuple-element.9) | copy-start | bytes 3500644
  54.4 4.8 %copy-start.2 = (f32[66,34,130]{2,1,0:T(8,128)}, f32[66,34,130]{2,1,0:T(8,128)S(1)}, u32[]{:S(2)}) copy-start(f32[66,34,130]{2,1,0:T(8,128)S(1)} %get-tuple-element.10) | copy-start | bytes 3500644
  59.3 12.0 %copy-start.4 = (f32[64,32,128]{2,1,0:T(8,128)}, f32[64,32,128]{2,1,0:T(8,128)S(1)}, u32[]{:S(2)}) copy-start(f32[64,32,128]{2,1,0:T(8,128)S(1)} %sqrt_add_fusion) | copy-start | bytes 3145732
  59.3 12.0 %collective-permute-start.6 = (f32[1,32,128]{2,1,0:T(8,128)S(1)}, f32[1,32,128]{2,1,0:T(8,128)S(1)}, u32[]{:S(2)}, u32[]{:S(2)}) collective-permute-start(f32[1,32,128]{2,1,0:T(8,128)S(1)} %get-tuple-element.20), channel_id=1, source_target_pairs={{16,0},{32,16},{48,32},{64,48},{80,64},{96,80},{112,96},{128,112},... | collective-permute-start | bytes 49160 | tf_op jit(solution)/shard_map/ppermute | solution.py:17
  61.2 10.1 %collective-permute-start.7 = (f32[1,32,128]{2,1,0:T(8,128)S(1)}, f32[1,32,128]{2,1,0:T(8,128)S(1)}, u32[]{:S(2)}, u32[]{:S(2)}) collective-permute-start(f32[1,32,128]{2,1,0:T(8,128)S(1)} %get-tuple-element.19), channel_id=1, source_target_pairs={{0,16},{16,32},{32,48},{48,64},{64,80},{80,96},{96,112},{112,128},... | collective-permute-start | bytes 49160 | tf_op jit(solution)/shard_map/ppermute | solution.py:14
  75.0 7.8 %collective-permute-start.8 = (f32[66,32,1]{0,1,2:T(8,128)S(1)}, f32[66,32,1]{0,1,2:T(8,128)S(1)}, u32[]{:S(2)}, u32[]{:S(2)}) collective-permute-start(f32[66,32,1]{0,1,2:T(8,128)S(1)} %copy.33), channel_id=1, source_target_pairs={{4,0},{8,4},{12,8},{5,1},{9,5},{13,9},{6,2},{10,6},{14,10},{7,3},{... | collective-permute-start | bytes 25352 | tf_op jit(solution)/shard_map/ppermute | solution.py:17
  76.3 17.5 %copy-start.15 = (s32[1,1,1,2]{3,2,1,0:T(1,128)S(1)}, s32[1,1,1,2]{3,2,1,0:T(1,128)}, u32[]{:S(2)}) copy-start(s32[1,1,1,2]{3,2,1,0:T(1,128)} %param.6) | copy-start | bytes 28
  78.2 6.6 %collective-permute-start.9 = (f32[66,32,1]{0,1,2:T(8,128)S(1)}, f32[66,32,1]{0,1,2:T(8,128)S(1)}, u32[]{:S(2)}, u32[]{:S(2)}) collective-permute-start(f32[66,32,1]{0,1,2:T(8,128)S(1)} %copy.35), channel_id=1, source_target_pairs={{0,4},{4,8},{8,12},{1,5},{5,9},{9,13},{2,6},{6,10},{10,14},{3,7},{... | collective-permute-start | bytes 25352 | tf_op jit(solution)/shard_map/ppermute | solution.py:14
  88.5 14.2 %collective-permute-start.10 = (f32[66,1,130]{2,1,0:T(1,128)S(1)}, f32[66,1,130]{2,1,0:T(1,128)S(1)}, u32[]{:S(2)}, u32[]{:S(2)}) collective-permute-start(f32[66,1,130]{2,1,0:T(1,128)S(1)} %get-tuple-element.12), channel_id=1, source_target_pairs={{1,0},{2,1},{3,2},{5,4},{6,5},{7,6},{9,8},{10,9},{11,10},{13,12},{... | collective-permute-start | bytes 102968 | tf_op jit(solution)/shard_map/ppermute | solution.py:17
  89.8 12.9 %collective-permute-start.11 = (f32[66,1,130]{2,1,0:T(1,128)S(1)}, f32[66,1,130]{2,1,0:T(1,128)S(1)}, u32[]{:S(2)}, u32[]{:S(2)}) collective-permute-start(f32[66,1,130]{2,1,0:T(1,128)S(1)} %get-tuple-element.11), channel_id=1, source_target_pairs={{0,1},{1,2},{2,3},{4,5},{5,6},{6,7},{8,9},{9,10},{10,11},{12,13},{... | collective-permute-start | bytes 102968 | tf_op jit(solution)/shard_map/ppermute | solution.py:14
  95.1 39.9 %all-to-all-start = ((f32[16,4,1152]{2,1,0:T(4,128)}), f32[16,4,1152]{2,1,0:T(4,128)S(1)}, u32[]{:S(2)}, u32[]{:S(2)}) async-start(f32[16,4,1152]{2,1,0:T(4,128)} %copy.40), calls=%async_computation | async-start | bytes 589824 | tf_op jit(solution)/shard_map/all_to_all | solution.py:98
  102.7 18.0 %copy-start.1 = (f32[66,34,130]{2,1,0:T(8,128)S(1)}, f32[66,34,130]{2,1,0:T(8,128)}, u32[]{:S(2)}) copy-start(f32[66,34,130]{2,1,0:T(8,128)} %copy-done) | copy-start | bytes 3500644
  102.7 18.0 %copy-start.3 = (f32[66,34,130]{2,1,0:T(8,128)S(1)}, f32[66,34,130]{2,1,0:T(8,128)}, u32[]{:S(2)}) copy-start(f32[66,34,130]{2,1,0:T(8,128)} %copy-done.2) | copy-start | bytes 3500644
  102.7 18.0 %copy-start.5 = (f32[64,32,128]{2,1,0:T(8,128)S(1)}, f32[64,32,128]{2,1,0:T(8,128)}, u32[]{:S(2)}) copy-start(f32[64,32,128]{2,1,0:T(8,128)} %copy-done.4) | copy-start | bytes 3145732
  102.7 18.0 %copy-start.8 = (f32[66,32,1]{2,1,0:T(8,128)S(1)}, f32[66,32,1]{2,1,0:T(8,128)}, u32[]{:S(2)}) copy-start(f32[66,32,1]{2,1,0:T(8,128)} %copy.34) | copy-start | bytes 25348
  102.7 18.0 %copy-start.9 = (f32[66,32,1]{2,1,0:T(8,128)S(1)}, f32[66,32,1]{2,1,0:T(8,128)}, u32[]{:S(2)}) copy-start(f32[66,32,1]{2,1,0:T(8,128)} %copy.36) | copy-start | bytes 25348
  227.6 4.0 %copy-start.14 = (f32[64,1152]{1,0:T(8,128)}, f32[64,1152]{1,0:T(8,128)S(1)}, u32[]{:S(2)}) copy-start(f32[64,1152]{1,0:T(8,128)S(1)} %reshape.53) | copy-start | bytes 884740
  233.1 1.2 copy-start.11
  233.2 1.5 copy-start.12
  233.2 1.8 copy-start.13
where the time goes:
time: 238 us; the launch traced here: 237 us
  blocking collectives  91.7 us (39%)
  other arithmetic  49.5 us (21%)
  starting transfers between devices  42.1 us (18%)
  local copies, waits for them, and re-layouts  35.2 us (15%)
  matrix products  11.5 us (5%)
  waiting for transfers between devices  6.24 us (3%)
    psum x1, blocking collectives, body(): owned = lax.psum(jnp.sum(received, axis=0), ('gy', 'gz'))  59.5 us
    all_gather x1, blocking collectives, body(): lax.all_gather(actuate(owned, owned_coef), 'gx', axis=0, tiled=True)  32.2 us
    another operation x3, other arithmetic, advance(): return jnp.stack(result)  32.2 us
    ppermute x6, starting transfers between devices, padded_2(): lax.ppermute(lax.slice_in_dim(block, block.shape[dim] - width, None, axis...  25.5 us
    slice x5, local copies, waits for them, and re-layouts, padded_2(): lax.slice_in_dim(block, block.shape[dim] - width, None, axis=dim)  10.3 us
    ppermute x6, starting transfers between devices, padded_2(): lax.ppermute(lax.slice_in_dim(block, 0, width, axis=dim), axis, backward)  8.99 us
    all_to_all x1, starting transfers between devices, body(): lax.all_to_all(partial_sample.reshape(rows, per_row, -1), 'gx', split_axi...  7.6 us
    concatenate x3, other arithmetic, padded_2(): block = jnp.concatenate([low, block, high], axis=dim)  5.95 us
  transfers between devices with their start and end apart: 13, of which 3 were waited for; matrix products, arithmetic and copies ran while one was open for 23% of the time, Pallas kernels for 0%

commit v1 on v0

--- a/solution.py
+++ b/solution.py
@@ -4,6 +4,10 @@
 from jax.sharding import PartitionSpec as P
 
 DIRS = (-3, -1, -2)
+
+
+def carry_task(message):
+    return jnp.sum(lax.all_gather(message, ("gy", "gz")), 0)
 
 
 def padded_2(block, sides, width):
@@ -98,7 +102,7 @@
     received = lax.all_to_all(
         partial_sample.reshape(rows, per_row, -1), "gx", split_axis=0, concat_axis=0, tiled=True
     )
-    owned = lax.psum(jnp.sum(received, axis=0), ("gy", "gz"))
+    owned = carry_task(jnp.sum(received, axis=0))
     owned_coef = lax.dynamic_slice_in_dim(chord, lax.axis_index("gx") * per_row, per_row, 0)
     forces = lax.all_gather(actuate(owned, owned_coef), "gx", axis=0, tiled=True)
     tile_force = jnp.dot(owning_block, forces, precision=lax.Precision.HIGHEST).astype(jnp.bfloat16)

time: 238 us -> 190 us (0.80)
  blocking collectives: 91.7 us -> 43.1 us
    psum x1 -> x0, blocking collectives: 59.5 us -> none  [body(): owned = lax.psum(jnp.sum(received, axis=0), ('gy', 'gz'))]
    all_gather x0 -> x1, blocking collectives: none -> 19.7 us  [carry_task(): return jnp.sum(lax.all_gather(message, ('gy', 'gz')), 0)]
    all_gather x1, blocking collectives: 32.2 us -> 23.4 us  [body(): lax.all_gather(actuate(owned, owned_coef), 'gx', axis=0, tiled=True)]
  transfers between devices with their start and end apart: 13 -> 13, of which waited for: 3 -> 3; matrix products, arithmetic and copies ran while one was open for 23% -> 29% of each run, Pallas kernels for 0% -> 0%
where the time goes in v1:
time: 190 us; the launch traced here: 189 us
  other arithmetic  49.6 us (26%)
  blocking collectives  43.1 us (23%)
  starting transfers between devices  42.1 us (22%)
  local copies, waits for them, and re-layouts  35.2 us (19%)
  matrix products  11.5 us (6%)
  waiting for transfers between devices  6.24 us (3%)
    another operation x3, other arithmetic, advance(): return jnp.stack(result)  32.2 us
    ppermute x6, starting transfers between devices, padded_2(): lax.ppermute(lax.slice_in_dim(block, block.shape[dim] - width, None, axis...  25.5 us
    all_gather x1, blocking collectives, body(): lax.all_gather(actuate(owned, owned_coef), 'gx', axis=0, tiled=True)  23.4 us
    all_gather x1, blocking collectives, carry_task(): return jnp.sum(lax.all_gather(message, ('gy', 'gz')), 0)  19.7 us
    slice x5, local copies, waits for them, and re-layouts, padded_2(): lax.slice_in_dim(block, block.shape[dim] - width, None, axis=dim)  10.3 us
    ppermute x6, starting transfers between devices, padded_2(): lax.ppermute(lax.slice_in_dim(block, 0, width, axis=dim), axis, backward)  8.99 us
    all_to_all x1, starting transfers between devices, body(): lax.all_to_all(partial_sample.reshape(rows, per_row, -1), 'gx', split_axi...  7.6 us
    concatenate x3, other arithmetic, padded_2(): block = jnp.concatenate([low, block, high], axis=dim)  5.95 us
  transfers between devices with their start and end apart: 13, of which 3 were waited for; matrix products, arithmetic and copies ran while one was open for 29% of the time, Pallas kernels for 0%

profile of v1, /device:TPU:1, one launch (start us, length us, event | category | flops | bytes accessed | tf_op | source)
XLA Modules:
  0.0 188.9 jit_solution(7824118150780139517)
XLA Ops:
  0.6 0.8 fusion.31
  1.5 4.9 %collective-permute-start = (f32[3,1,32,128]{3,2,1,0:T(8,128)S(1)}, f32[3,1,32,128]{3,2,1,0:T(8,128)S(1)}, u32[]{:S(2)}, u32[]{:S(2)}) collective-permute-start(f32[3,1,32,128]{3,2,1,0:T(8,128)S(1)} %get-tuple-element.16), channel_id=1, source_target_pairs={{0,16},{16,32},{32,48},{48,64},{64,80},{80,96},{96,112},{112,128},... | collective-permute-start | bytes 147464 | tf_op jit(solution)/shard_map/ppermute | solution.py:18
  6.4 1.9 %collective-permute-start.1 = (f32[3,1,32,128]{3,2,1,0:T(8,128)S(1)}, f32[3,1,32,128]{3,2,1,0:T(8,128)S(1)}, u32[]{:S(2)}, u32[]{:S(2)}) collective-permute-start(f32[3,1,32,128]{3,2,1,0:T(8,128)S(1)} %get-tuple-element.15), channel_id=1, source_target_pairs={{16,0},{32,16},{48,32},{64,48},{80,64},{96,80},{112,96},{128,112},... | collective-permute-start | bytes 147464 | tf_op jit(solution)/shard_map/ppermute | solution.py:21
  8.3 2.2 %constant_dynamic-update-slice_fusion.1 = f32[3,66,32,128]{3,2,1,0:T(8,128)S(1)} fusion(f32[3,66,32,128]{3,2,1,0:T(8,128)S(1)} %constant_dynamic-update-slice_fusion.2, f32[3,64,32,128]{3,2,1,0:T(8,128)} %param.5), kind=kLoop, calls=%fused_computation.71 | loop fusion | bytes 6291456
  10.5 1.3 collective-permute-done.1
  11.8 3.9 %fusion.30 = (f32[3,66,32,1]{3,2,1,0:T(8,128)}, f32[3,66,32,1]{3,2,1,0:T(8,128)}) fusion(f32[3,66,32,128]{3,2,1,0:T(8,128)S(1)} %constant_dynamic-update-slice_fusion), kind=kLoop, calls=%fused_computation.87 | loop fusion | bytes 101376 | tf_op jit(solution)/shard_map/slice | solution.py:19
  15.7 2.8 %copy.29 = f32[3,66,32,1]{1,2,3,0:T(8,128)S(1)} copy(f32[3,66,32,1]{3,2,1,0:T(8,128)} %get-tuple-element.13) | data formatting | bytes 50688 | tf_op jit(solution)/shard_map/slice | solution.py:19
  18.5 3.1 %collective-permute-start.2 = (f32[3,66,32,1]{1,2,3,0:T(8,128)S(1)}, f32[3,66,32,1]{1,2,3,0:T(8,128)S(1)}, u32[]{:S(2)}, u32[]{:S(2)}) collective-permute-start(f32[3,66,32,1]{1,2,3,0:T(8,128)S(1)} %copy.29), channel_id=1, source_target_pairs={{0,4},{4,8},{8,12},{1,5},{5,9},{9,13},{2,6},{6,10},{10,14},{3,7},{... | collective-permute-start | bytes 76040 | tf_op jit(solution)/shard_map/ppermute | solution.py:18
  21.6 2.8 %copy.30 = f32[3,66,32,1]{1,2,3,0:T(8,128)S(1)} copy(f32[3,66,32,1]{3,2,1,0:T(8,128)} %get-tuple-element.14) | data formatting | bytes 50688 | tf_op jit(solution)/shard_map/slice | solution.py:21
  24.4 1.3 collective-permute-start.3
  25.7 4.6 %reshape.47 = f32[3,64,4096]{2,1,0:T(8,128)} reshape(f32[3,64,32,128]{3,2,1,0:T(8,128)} %param.5) | data formatting | bytes 6291456 | tf_op jit(solution)/shard_map/reshape | solution.py:83
  30.3 2.7 %copy.31 = f32[3,66,32,1]{3,2,1,0:T(8,128)} copy(f32[3,66,32,1]{1,2,3,0:T(8,128)S(1)} %collective-permute-done.2) | data formatting | bytes 50688 | tf_op jit(solution)/shard_map/ppermute | solution.py:18
  33.0 2.7 %copy.32 = f32[3,66,32,1]{3,2,1,0:T(8,128)} copy(f32[3,66,32,1]{1,2,3,0:T(8,128)S(1)} %collective-permute-done.3) | data formatting | bytes 50688 | tf_op jit(solution)/shard_map/ppermute | solution.py:21
  35.7 3.4 %pad_maximum_fusion.22 = (f32[3,66,1,130]{3,2,1,0:T(1,128)S(1)}, f32[3,66,1,130]{3,2,1,0:T(1,128)S(1)}) fusion(f32[3,66,32,1]{3,2,1,0:T(8,128)} %copy.32, f32[3,66,32,128]{3,2,1,0:T(8,128)S(1)} %constant_dynamic-update-slice_fusion, f32[3,66,32,1]{3,2,1,0:T(8,128)} %copy.31), kind=kLoop, calls=%fused_computation.60 | loop fusion | flops 102960 | bytes 3500640 | tf_op jit(solution)/shard_map/slice | solution.py:19
  39.1 3.3 %collective-permute-start.4 = (f32[3,66,1,130]{3,2,1,0:T(1,128)S(1)}, f32[3,66,1,130]{3,2,1,0:T(1,128)S(1)}, u32[]{:S(2)}, u32[]{:S(2)}) collective-permute-start(f32[3,66,1,130]{3,2,1,0:T(1,128)S(1)} %get-tuple-element.6), channel_id=1, source_target_pairs={{0,1},{1,2},{2,3},{4,5},{5,6},{6,7},{8,9},{9,10},{10,11},{12,13},{... | collective-permute-start | bytes 308888 | tf_op jit(solution)/shard_map/ppermute | solution.py:18
  42.5 1.3 collective-permute-start.5
  43.8 1.1 convolution_convert_fusion
  44.9 0.9 collective-permute-done.4
  45.8 4.1 %collective-permute-done.5 = f32[3,66,1,130]{3,2,1,0:T(1,128)S(1)} collective-permute-done((f32[3,66,1,130]{3,2,1,0:T(1,128)S(1)}, f32[3,66,1,130]{3,2,1,0:T(1,128)S(1)}, u32[]{:S(2)}, u32[]{:S(2)}) %collective-permute-start.5) | collective-permute-done | bytes 102992 | tf_op jit(solution)/shard_map/ppermute | solution.py:21
  49.9 4.0 %pad_maximum_fusion = f32[3,66,34,130]{3,2,1,0:T(8,128)S(1)} fusion(f32[3,66,1,130]{3,2,1,0:T(1,128)S(1)} %collective-permute-done.5, f32[3,66,32,1]{3,2,1,0:T(8,128)S(1)} %copy-done.7, f32[3,66,32,128]{3,2,1,0:T(8,128)S(1)} %constant_dynamic-update-slice_fusion, f32[3,66,32,1]{3,2,1,0:T(8,128)S(1)} %copy-done.6, f32[3,66,1,130]{3,2,1,0:T(1,128)S(1)} %collective-permute-done.4), kind=kLoop, calls=%fused_computation | loop fusion | flops 3500640 | bytes 7001280 | tf_op jit(solution)/shard_map/concatenate | solution.py:22
  53.9 0.5 slice_bitcast_fusion.1
  54.5 4.8 %sqrt_add_fusion = f32[64,32,128]{2,1,0:T(8,128)S(1)} fusion(f32[66,34,130]{2,1,0:T(8,128)S(1)} %get-tuple-element.10, f32[66,34,130]{2,1,0:T(8,128)S(1)} %get-tuple-element.8, f32[66,34,130]{2,1,0:T(8,128)S(1)} %get-tuple-element.9), kind=kLoop, calls=%fused_computation.45 | loop fusion | flops 9961472 | bytes 19922944 | tf_op jit(solution)/shard_map/add | solution.py:43
  59.3 1.9 %collective-permute-start.6 = (f32[1,32,128]{2,1,0:T(8,128)S(1)}, f32[1,32,128]{2,1,0:T(8,128)S(1)}, u32[]{:S(2)}, u32[]{:S(2)}) collective-permute-start(f32[1,32,128]{2,1,0:T(8,128)S(1)} %get-tuple-element.20), channel_id=1, source_target_pairs={{16,0},{32,16},{48,32},{64,48},{80,64},{96,80},{112,96},{128,112},... | collective-permute-start | bytes 49160 | tf_op jit(solution)/shard_map/ppermute | solution.py:21
  61.2 5.5 %collective-permute-start.7 = (f32[1,32,128]{2,1,0:T(8,128)S(1)}, f32[1,32,128]{2,1,0:T(8,128)S(1)}, u32[]{:S(2)}, u32[]{:S(2)}) collective-permute-start(f32[1,32,128]{2,1,0:T(8,128)S(1)} %get-tuple-element.19), channel_id=1, source_target_pairs={{0,16},{16,32},{32,48},{48,64},{64,80},{80,96},{96,112},{112,128},... | collective-permute-start | bytes 49160 | tf_op jit(solution)/shard_map/ppermute | solution.py:18
  66.8 4.5 %fusion.2 = f32[2,3,384]{2,1,0:T(4,128)S(1)} fusion(bf16[1,1,1,2,384,4096]{5,4,3,2,1,0:T(8,128)(2,1)} %param.8, bf16[2,3,4096]{2,0,1:T(2,128)(2,1)S(1)} %convolution_convert_fusion), kind=kOutput, calls=%fused_computation.3 | convolution fusion | flops 18874368 | bytes 6349824 | tf_op jit(solution)/shard_map/spq,scq->scp/dot_general | solution.py:88
  71.4 1.7 fusion.32
  73.1 1.9 copy.33
  75.0 1.3 collective-permute-start.8
  76.3 1.9 copy.35
  78.2 4.6 %collective-permute-start.9 = (f32[66,32,1]{0,1,2:T(8,128)S(1)}, f32[66,32,1]{0,1,2:T(8,128)S(1)}, u32[]{:S(2)}, u32[]{:S(2)}) collective-permute-start(f32[66,32,1]{0,1,2:T(8,128)S(1)} %copy.35), channel_id=1, source_target_pairs={{0,4},{4,8},{8,12},{1,5},{5,9},{9,13},{2,6},{6,10},{10,14},{3,7},{... | collective-permute-start | bytes 25352 | tf_op jit(solution)/shard_map/ppermute | solution.py:18
  82.8 1.9 %copy.34 = f32[66,32,1]{2,1,0:T(8,128)} copy(f32[66,32,1]{0,1,2:T(8,128)S(1)} %collective-permute-done.8) | data formatting | bytes 16896 | tf_op jit(solution)/shard_map/ppermute | solution.py:21
  84.7 1.9 %copy.36 = f32[66,32,1]{2,1,0:T(8,128)} copy(f32[66,32,1]{0,1,2:T(8,128)S(1)} %collective-permute-done.9) | data formatting | bytes 16896 | tf_op jit(solution)/shard_map/ppermute | solution.py:18
  86.6 1.9 pad_maximum_fusion.23
  88.5 1.3 collective-permute-start.10
  89.8 4.0 %collective-permute-start.11 = (f32[66,1,130]{2,1,0:T(1,128)S(1)}, f32[66,1,130]{2,1,0:T(1,128)S(1)}, u32[]{:S(2)}, u32[]{:S(2)}) collective-permute-start(f32[66,1,130]{2,1,0:T(1,128)S(1)} %get-tuple-element.11), channel_id=1, source_target_pairs={{0,1},{1,2},{2,3},{4,5},{5,6},{6,7},{8,9},{9,10},{10,11},{12,13},{... | collective-permute-start | bytes 102968 | tf_op jit(solution)/shard_map/ppermute | solution.py:18
  94.2 0.8 copy.40
  95.1 7.6 %all-to-all-start = ((f32[16,4,1152]{2,1,0:T(4,128)}), f32[16,4,1152]{2,1,0:T(4,128)S(1)}, u32[]{:S(2)}, u32[]{:S(2)}) async-start(f32[16,4,1152]{2,1,0:T(4,128)} %copy.40), calls=%async_computation | async-start | bytes 589824 | tf_op jit(solution)/shard_map/all_to_all | solution.py:102
  102.7 17.9 %add_bitcast_fusion.2 = f32[1,64,32,128]{3,2,1,0:T(8,128)} fusion(f32[66,34,130]{2,1,0:T(8,128)} %copy-done.2, f32[66,34,130]{2,1,0:T(8,128)S(1)} %get-tuple-element.8, f32[66,34,130]{2,1,0:T(8,128)} %copy-done, f32[64,32,128]{2,1,0:T(8,128)} %copy-done.4, f32[1,32,128]{2,1,0:T(8,128)S(1)} %collective-permute-done.6, ...), kind=kLoop, calls=%fused_computation.44 | loop fusion | flops 15990784 | bytes 11652640 | tf_op jit(solution)/shard_map/stack | solution.py:61
  120.7 7.1 %add_bitcast_fusion.1 = f32[1,64,32,128]{3,2,1,0:T(8,128)} fusion(f32[66,34,130]{2,1,0:T(8,128)S(1)} %get-tuple-element.8, f32[66,34,130]{2,1,0:T(8,128)S(1)} %copy-done.3, f32[66,34,130]{2,1,0:T(8,128)S(1)} %copy-done.1, f32[64,32,128]{2,1,0:T(8,128)S(1)} %copy-done.5, f32[1,32,128]{2,1,0:T(8,128)S(1)} %collective-permute-done.6, ...), kind=kLoop, calls=%fused_computation.43 | loop fusion | flops 15990784 | bytes 11652640 | tf_op jit(solution)/shard_map/stack | solution.py:61
  127.9 7.1 %add_bitcast_fusion = f32[1,64,32,128]{3,2,1,0:T(8,128)} fusion(f32[66,34,130]{2,1,0:T(8,128)S(1)} %copy-done.1, f32[66,34,130]{2,1,0:T(8,128)S(1)} %copy-done.3, f32[66,34,130]{2,1,0:T(8,128)S(1)} %get-tuple-element.8, f32[64,32,128]{2,1,0:T(8,128)S(1)} %copy-done.5, f32[1,32,128]{2,1,0:T(8,128)S(1)} %collective-permute-done.6, ...), kind=kLoop, calls=%fused_computation.42 | loop fusion | flops 15990784 | bytes 11652640 | tf_op jit(solution)/shard_map/stack | solution.py:61
  135.0 19.7 %all-gather.1 = f32[16,4,1152]{2,1,0:T(4,128)S(1)} all-gather(f32[1,4,1152]{2,1,0:T(4,128)S(1)} %bitcast.44), channel_id=2, replica_groups=mesh['gx'=16,'gy'=4,'gz'=4] {'gy','gz'}, dimensions={0}, use_global_device_ids=true | all-gather | bytes 313344 | tf_op jit(solution)/shard_map/all_gather | solution.py:10
  154.8 0.7 sqrt_multiply_fusion
  155.6 23.4 %all-gather.2 = f32[16,4,1152]{2,1,0:T(4,128)S(1)} all-gather(f32[1,4,1152]{2,1,0:T(4,128)S(1)} %multiply_bitcast_fusion), channel_id=1, replica_groups=mesh['gx'=16,'gy'=4,'gz'=4] {'gx'}, dimensions={0}, use_global_device_ids=true | all-gather | bytes 313344 | tf_op jit(solution)/shard_map/all_gather | solution.py:107
  179.3 3.7 %fusion = f32[2,3,4096]{2,1,0:T(4,128)S(1)} fusion(bf16[2,3,384]{2,1,0:T(4,128)(2,1)S(1)} %reshape.50, bf16[1,1,1,2,384,4096]{5,4,3,2,1,0:T(8,128)(2,1)} %param.8), kind=kOutput, calls=%fused_computation.1 | convolution fusion | flops 18874368 | bytes 6394368 | tf_op jit(solution)/shard_map/axz,ahx->ahz/dot_general | solution.py:109
  183.1 1.5 fusion.16
  184.6 0.5 copy.42
  185.2 0.6 copy-done.11
  186.4 2.4 %bitcast_add_fusion = f32[3,64,32,128]{3,2,1,0:T(8,128)} fusion(f32[1,64,32,128]{3,2,1,0:T(8,128)S(1)} %copy-done.13, f32[1,64,32,128]{3,2,1,0:T(8,128)S(1)} %copy-done.12, f32[1,64,32,128]{3,2,1,0:T(8,128)S(1)} %copy-done.11, f32[3,64,32,128]{3,2,1,0:T(8,128)S(1)} %bitcast.43), kind=kLoop, calls=%fused_computation.6 | loop fusion | flops 2359296 | bytes 9437184 | tf_op jit(solution)/shard_map/add | solution.py:121
  (59 shorter events, 1.8 us)
Async XLA Ops:
  1.5 6.9 %collective-permute-start = (f32[3,1,32,128]{3,2,1,0:T(8,128)S(1)}, f32[3,1,32,128]{3,2,1,0:T(8,128)S(1)}, u32[]{:S(2)}, u32[]{:S(2)}) collective-permute-start(f32[3,1,32,128]{3,2,1,0:T(8,128)S(1)} %get-tuple-element.16), channel_id=1, source_target_pairs={{0,16},{16,32},{32,48},{48,64},{64,80},{80,96},{96,112},{112,128},... | collective-permute-start | bytes 147464 | tf_op jit(solution)/shard_map/ppermute | solution.py:18
  6.4 5.4 %collective-permute-start.1 = (f32[3,1,32,128]{3,2,1,0:T(8,128)S(1)}, f32[3,1,32,128]{3,2,1,0:T(8,128)S(1)}, u32[]{:S(2)}, u32[]{:S(2)}) collective-permute-start(f32[3,1,32,128]{3,2,1,0:T(8,128)S(1)} %get-tuple-element.15), channel_id=1, source_target_pairs={{16,0},{32,16},{48,32},{64,48},{80,64},{96,80},{112,96},{128,112},... | collective-permute-start | bytes 147464 | tf_op jit(solution)/shard_map/ppermute | solution.py:21
  18.5 11.8 %collective-permute-start.2 = (f32[3,66,32,1]{1,2,3,0:T(8,128)S(1)}, f32[3,66,32,1]{1,2,3,0:T(8,128)S(1)}, u32[]{:S(2)}, u32[]{:S(2)}) collective-permute-start(f32[3,66,32,1]{1,2,3,0:T(8,128)S(1)} %copy.29), channel_id=1, source_target_pairs={{0,4},{4,8},{8,12},{1,5},{5,9},{9,13},{2,6},{6,10},{10,14},{3,7},{... | collective-permute-start | bytes 76040 | tf_op jit(solution)/shard_map/ppermute | solution.py:18
  24.4 8.6 %collective-permute-start.3 = (f32[3,66,32,1]{1,2,3,0:T(8,128)S(1)}, f32[3,66,32,1]{1,2,3,0:T(8,128)S(1)}, u32[]{:S(2)}, u32[]{:S(2)}) collective-permute-start(f32[3,66,32,1]{1,2,3,0:T(8,128)S(1)} %copy.30), channel_id=1, source_target_pairs={{4,0},{8,4},{12,8},{5,1},{9,5},{13,9},{6,2},{10,6},{14,10},{7,3},{... | collective-permute-start | bytes 76040 | tf_op jit(solution)/shard_map/ppermute | solution.py:21
  35.7 8.1 %copy-start.10 = (f32[3,64,4096]{2,1,0:T(8,128)S(1)}, f32[3,64,4096]{2,1,0:T(8,128)}, u32[]{:S(2)}) copy-start(f32[3,64,4096]{2,1,0:T(8,128)} %reshape.47) | copy-start | bytes 9437188
  35.7 8.1 %copy-start.16 = (s32[1,1,1,2]{3,2,1,0:T(1,128)S(1)}, s32[1,1,1,2]{3,2,1,0:T(1,128)}, u32[]{:S(2)}) copy-start(s32[1,1,1,2]{3,2,1,0:T(1,128)} %param.7) | copy-start | bytes 28
  35.7 14.2 %copy-start.6 = (f32[3,66,32,1]{3,2,1,0:T(8,128)S(1)}, f32[3,66,32,1]{3,2,1,0:T(8,128)}, u32[]{:S(2)}) copy-start(f32[3,66,32,1]{3,2,1,0:T(8,128)} %copy.31) | copy-start | bytes 76036
  35.7 14.2 %copy-start.7 = (f32[3,66,32,1]{3,2,1,0:T(8,128)S(1)}, f32[3,66,32,1]{3,2,1,0:T(8,128)}, u32[]{:S(2)}) copy-start(f32[3,66,32,1]{3,2,1,0:T(8,128)} %copy.32) | copy-start | bytes 76036
  39.1 6.6 %collective-permute-start.4 = (f32[3,66,1,130]{3,2,1,0:T(1,128)S(1)}, f32[3,66,1,130]{3,2,1,0:T(1,128)S(1)}, u32[]{:S(2)}, u32[]{:S(2)}) collective-permute-start(f32[3,66,1,130]{3,2,1,0:T(1,128)S(1)} %get-tuple-element.6), channel_id=1, source_target_pairs={{0,1},{1,2},{2,3},{4,5},{5,6},{6,7},{8,9},{9,10},{10,11},{12,13},{... | collective-permute-start | bytes 308888 | tf_op jit(solution)/shard_map/ppermute | solution.py:18
  42.5 7.4 %collective-permute-start.5 = (f32[3,66,1,130]{3,2,1,0:T(1,128)S(1)}, f32[3,66,1,130]{3,2,1,0:T(1,128)S(1)}, u32[]{:S(2)}, u32[]{:S(2)}) collective-permute-start(f32[3,66,1,130]{3,2,1,0:T(1,128)S(1)} %get-tuple-element.7), channel_id=1, source_target_pairs={{1,0},{2,1},{3,2},{5,4},{6,5},{7,6},{9,8},{10,9},{11,10},{13,12},{... | collective-permute-start | bytes 308888 | tf_op jit(solution)/shard_map/ppermute | solution.py:21
  54.4 4.8 %copy-start = (f32[66,34,130]{2,1,0:T(8,128)}, f32[66,34,130]{2,1,0:T(8,128)S(1)}, u32[]{:S(2)}) copy-start(f32[66,34,130]{2,1,0:T(8,128)S(1)} %get-tuple-element.9) | copy-start | bytes 3500644
  54.4 4.8 %copy-start.2 = (f32[66,34,130]{2,1,0:T(8,128)}, f32[66,34,130]{2,1,0:T(8,128)S(1)}, u32[]{:S(2)}) copy-start(f32[66,34,130]{2,1,0:T(8,128)S(1)} %get-tuple-element.10) | copy-start | bytes 3500644
  59.3 12.0 %copy-start.4 = (f32[64,32,128]{2,1,0:T(8,128)}, f32[64,32,128]{2,1,0:T(8,128)S(1)}, u32[]{:S(2)}) copy-start(f32[64,32,128]{2,1,0:T(8,128)S(1)} %sqrt_add_fusion) | copy-start | bytes 3145732
  59.3 12.0 %collective-permute-start.6 = (f32[1,32,128]{2,1,0:T(8,128)S(1)}, f32[1,32,128]{2,1,0:T(8,128)S(1)}, u32[]{:S(2)}, u32[]{:S(2)}) collective-permute-start(f32[1,32,128]{2,1,0:T(8,128)S(1)} %get-tuple-element.20), channel_id=1, source_target_pairs={{16,0},{32,16},{48,32},{64,48},{80,64},{96,80},{112,96},{128,112},... | collective-permute-start | bytes 49160 | tf_op jit(solution)/shard_map/ppermute | solution.py:21
  61.2 10.1 %collective-permute-start.7 = (f32[1,32,128]{2,1,0:T(8,128)S(1)}, f32[1,32,128]{2,1,0:T(8,128)S(1)}, u32[]{:S(2)}, u32[]{:S(2)}) collective-permute-start(f32[1,32,128]{2,1,0:T(8,128)S(1)} %get-tuple-element.19), channel_id=1, source_target_pairs={{0,16},{16,32},{32,48},{48,64},{64,80},{80,96},{96,112},{112,128},... | collective-permute-start | bytes 49160 | tf_op jit(solution)/shard_map/ppermute | solution.py:18
  75.0 7.8 %collective-permute-start.8 = (f32[66,32,1]{0,1,2:T(8,128)S(1)}, f32[66,32,1]{0,1,2:T(8,128)S(1)}, u32[]{:S(2)}, u32[]{:S(2)}) collective-permute-start(f32[66,32,1]{0,1,2:T(8,128)S(1)} %copy.33), channel_id=1, source_target_pairs={{4,0},{8,4},{12,8},{5,1},{9,5},{13,9},{6,2},{10,6},{14,10},{7,3},{... | collective-permute-start | bytes 25352 | tf_op jit(solution)/shard_map/ppermute | solution.py:21
  76.3 17.5 %copy-start.15 = (s32[1,1,1,2]{3,2,1,0:T(1,128)S(1)}, s32[1,1,1,2]{3,2,1,0:T(1,128)}, u32[]{:S(2)}) copy-start(s32[1,1,1,2]{3,2,1,0:T(1,128)} %param.6) | copy-start | bytes 28
  78.2 6.6 %collective-permute-start.9 = (f32[66,32,1]{0,1,2:T(8,128)S(1)}, f32[66,32,1]{0,1,2:T(8,128)S(1)}, u32[]{:S(2)}, u32[]{:S(2)}) collective-permute-start(f32[66,32,1]{0,1,2:T(8,128)S(1)} %copy.35), channel_id=1, source_target_pairs={{0,4},{4,8},{8,12},{1,5},{5,9},{9,13},{2,6},{6,10},{10,14},{3,7},{... | collective-permute-start | bytes 25352 | tf_op jit(solution)/shard_map/ppermute | solution.py:18
  88.5 14.2 %collective-permute-start.10 = (f32[66,1,130]{2,1,0:T(1,128)S(1)}, f32[66,1,130]{2,1,0:T(1,128)S(1)}, u32[]{:S(2)}, u32[]{:S(2)}) collective-permute-start(f32[66,1,130]{2,1,0:T(1,128)S(1)} %get-tuple-element.12), channel_id=1, source_target_pairs={{1,0},{2,1},{3,2},{5,4},{6,5},{7,6},{9,8},{10,9},{11,10},{13,12},{... | collective-permute-start | bytes 102968 | tf_op jit(solution)/shard_map/ppermute | solution.py:21
  89.8 12.9 %collective-permute-start.11 = (f32[66,1,130]{2,1,0:T(1,128)S(1)}, f32[66,1,130]{2,1,0:T(1,128)S(1)}, u32[]{:S(2)}, u32[]{:S(2)}) collective-permute-start(f32[66,1,130]{2,1,0:T(1,128)S(1)} %get-tuple-element.11), channel_id=1, source_target_pairs={{0,1},{1,2},{2,3},{4,5},{5,6},{6,7},{8,9},{9,10},{10,11},{12,13},{... | collective-permute-start | bytes 102968 | tf_op jit(solution)/shard_map/ppermute | solution.py:18
  95.1 39.9 %all-to-all-start = ((f32[16,4,1152]{2,1,0:T(4,128)}), f32[16,4,1152]{2,1,0:T(4,128)S(1)}, u32[]{:S(2)}, u32[]{:S(2)}) async-start(f32[16,4,1152]{2,1,0:T(4,128)} %copy.40), calls=%async_computation | async-start | bytes 589824 | tf_op jit(solution)/shard_map/all_to_all | solution.py:102
  102.7 18.0 %copy-start.1 = (f32[66,34,130]{2,1,0:T(8,128)S(1)}, f32[66,34,130]{2,1,0:T(8,128)}, u32[]{:S(2)}) copy-start(f32[66,34,130]{2,1,0:T(8,128)} %copy-done) | copy-start | bytes 3500644
  102.7 18.0 %copy-start.3 = (f32[66,34,130]{2,1,0:T(8,128)S(1)}, f32[66,34,130]{2,1,0:T(8,128)}, u32[]{:S(2)}) copy-start(f32[66,34,130]{2,1,0:T(8,128)} %copy-done.2) | copy-start | bytes 3500644
  102.7 18.0 %copy-start.5 = (f32[64,32,128]{2,1,0:T(8,128)S(1)}, f32[64,32,128]{2,1,0:T(8,128)}, u32[]{:S(2)}) copy-start(f32[64,32,128]{2,1,0:T(8,128)} %copy-done.4) | copy-start | bytes 3145732
  102.7 18.0 %copy-start.8 = (f32[66,32,1]{2,1,0:T(8,128)S(1)}, f32[66,32,1]{2,1,0:T(8,128)}, u32[]{:S(2)}) copy-start(f32[66,32,1]{2,1,0:T(8,128)} %copy.34) | copy-start | bytes 25348
  102.7 18.0 %copy-start.9 = (f32[66,32,1]{2,1,0:T(8,128)S(1)}, f32[66,32,1]{2,1,0:T(8,128)}, u32[]{:S(2)}) copy-start(f32[66,32,1]{2,1,0:T(8,128)} %copy.36) | copy-start | bytes 25348
  179.1 4.0 %copy-start.14 = (f32[64,1152]{1,0:T(8,128)}, f32[64,1152]{1,0:T(8,128)S(1)}, u32[]{:S(2)}) copy-start(f32[64,1152]{1,0:T(8,128)S(1)} %reshape.56) | copy-start | bytes 884740
  184.6 1.2 copy-start.11
  184.6 1.5 copy-start.12
  184.6 1.8 copy-start.13
